TPU v7x, 32 devices: a whole 2x2x4 slice. The times are simulated.
32 devices in a mesh: grp: 2 (over x), dev: 16 (over z, y, core).
Axes of the slice: x: 2, y: 2, z: 4, core: 2. Of those that a mesh axis runs over, the one named last changes fastest.
Arguments:
- line_bin: int32 [65536], P(('grp', 'dev')), may hold values from 0 to 16383, as said below
- line_slot: int32 [65536], P(('grp', 'dev')), may hold values from 0 to 31
- strength: float32 [65536], P(('grp', 'dev')), may hold values from 0.05 to 1
- line_count: int32 [32], P(('grp', 'dev')), may hold values from 1024 to 2048
- gauss_width: float32 [32], replicated, may hold values from 2 to 40
- lorentz_width: float32 [32], replicated, may hold values from 1 to 30
- mixing: float32 [32], replicated, may hold values from 0.1 to 0.9
- profile_factor: float32 [32, 257], replicated, may hold values from 0.25 to 1.75
Outputs:
- spectrum: float32 [32768], P(('grp', 'dev'))
Inputs may be any that keep to these rules, and one draw needn't show every extreme that they name: `line_bin`: every line of device (g, d) (the d-th block of 2048 lines within the g-th group of 16 blocks) has a bin within (d - 2) * 1024 to (d + 3) * 1024 - 1 of its super-band.
All inputs are finite; a program needn't handle non-finite values.
Results may differ from a plain program's by a relative error of at most 0.00005.
Values sent between devices are 32-bit elements; how exact they have to be, the bound alone decides.
No kernel may reach another device: no remote copies, remote signals or barrier semaphores. Data moves between devices by JAX's collectives and lax.ppermute only.
A program may use at most 64 MiB of HBM per device.

v0:
```python
import jax
import jax.numpy as jnp
from jax import lax
from jax.experimental import pallas as pl
from jax.experimental.pallas import tpu as pltpu
from jax.sharding import PartitionSpec as P

HOP = 2
SPAN = 1024
LANES = 128
BLOCK = 128
STAGE = 512
AXES = ("grp", "dev")


def column(row):
    n = row.shape[1]
    here = lax.broadcasted_iota(jnp.int32, (n, n), 0)
    there = lax.broadcasted_iota(jnp.int32, (n, n), 1)
    return jnp.sum(jnp.where(here == there, row, 0.0), axis=1, keepdims=True)


def halves(value):
    high = value.astype(jnp.bfloat16)
    low = (value - high.astype(jnp.float32)).astype(jnp.bfloat16)
    return high, low


def pick_lanes(value, index):
    numbers = lax.GatherDimensionNumbers(
        offset_dims=(),
        collapsed_slice_dims=(1,),
        start_index_map=(1,),
        operand_batching_dims=(0,),
        start_indices_batching_dims=(0,),
    )
    return lax.gather(
        value, index[..., None], numbers, (1, 1), mode=lax.GatherScatterMode.PROMISE_IN_BOUNDS
    )


def kernel_table(gauss, lorentz, mixing, factor_ref):
    slots = gauss.shape[0]
    wing = (factor_ref.shape[1] - 1) // 2

    def profile(offset, factor):
        square = offset * offset
        width = lorentz * lorentz
        shape = mixing * (width / (square + width)) + (1.0 - mixing) * jnp.exp(
            -square / (2.0 * gauss * gauss)
        )
        return shape * factor

    lane = lax.broadcasted_iota(jnp.int32, (slots, LANES), 1)
    raw = []
    for start in range(0, 2 * wing, LANES):
        offset = (lane + (start - wing)).astype(jnp.float32)
        raw.append(profile(offset, factor_ref[:, start : start + LANES]))
    last = profile(jnp.full((slots, 1), float(wing), jnp.float32), factor_ref[:, 2 * wing :])
    total = jnp.sum(sum(raw), axis=1, keepdims=True) + last
    return jnp.concatenate(raw, axis=1) / total, last / total


def deposit_kernel(
    count_ref, bin_ref, slot_ref, strength_ref, gauss_ref, lorentz_ref, mixing_ref, factor_ref, give_ref, half_ref, acc_ref, spread_ref
):
    slots = gauss_ref.shape[1]
    pieces = (factor_ref.shape[1] - 1) // LANES
    lines = bin_ref.shape[1]
    reach_rows = (2 * HOP + 1) * SPAN // LANES
    rows = -(-reach_rows // 16) * 16
    bf16 = jnp.bfloat16

    table, last = kernel_table(
        column(gauss_ref[...]), column(lorentz_ref[...]), column(mixing_ref[...]), factor_ref
    )
    high, low = halves(table)
    weights = jnp.concatenate([high, low, high], axis=0)
    aux = lax.broadcasted_iota(jnp.int32, (16, LANES), 0)
    aux_lane = lax.broadcasted_iota(jnp.int32, (16, LANES), 1)
    steps = jnp.where(aux == 0, 1, jnp.where(aux == 1, LANES - aux_lane, 0))
    steps = steps.astype(jnp.float32).astype(bf16)
    weights = jnp.concatenate(
        [
            jnp.concatenate([weights, jnp.zeros((3 * slots, LANES), bf16)], axis=1),
            jnp.concatenate([jnp.zeros((16, table.shape[1]), bf16), steps], axis=1),
        ],
        axis=0,
    )

    anchor = (lax.axis_index("dev") - HOP) * SPAN
    count = count_ref[0]
    slot_ids = lax.broadcasted_iota(jnp.int32, (slots, STAGE), 0)
    row_ids = lax.broadcasted_iota(jnp.int32, (rows, BLOCK), 0)
    aux_ids = lax.broadcasted_iota(jnp.int32, (16, STAGE), 0)
    zero, one = jnp.zeros((BLOCK, LANES), bf16), jnp.ones((BLOCK, LANES), bf16)
    ends_at = []
    for start in range(0, lines, STAGE):
        at = slice(start, start + STAGE)
        col = (bin_ref[:, at] - anchor) & (LANES - 1)
        live = lax.broadcasted_iota(jnp.int32, (1, STAGE), 1) + start < count
        weight = jnp.where(live, strength_ref[:, at], 0.0)
        chosen = jnp.where(slot_ids == slot_ref[:, at], weight, 0.0)
        ends_at.append(jnp.sum(chosen * last, axis=0, keepdims=True))
        chosen_high, chosen_low = halves(chosen)
        aux = jnp.where(aux_ids == 0, col, jnp.where(aux_ids == 1, 1, 0))
        aux = aux.astype(jnp.float32).astype(bf16)
        picks = jnp.concatenate([chosen_high, chosen_high, chosen_low, aux], axis=0)
        spread_ref[at, :] = lax.dot_general(
            picks, weights, (((0,), (0,)), ((), ())), preferred_element_type=jnp.float32
        )
    ends_at = jnp.concatenate(ends_at, axis=1)
    acc = jnp.zeros((rows, 2 * (pieces + 1) * LANES), jnp.float32)
    ends = jnp.zeros((2 * rows, LANES), jnp.float32)
    for start in range(0, lines, BLOCK):
        at = slice(start, start + BLOCK)
        row = (bin_ref[:, at] - anchor) >> 7
        step = spread_ref[at, pieces * LANES :]
        index = step.astype(jnp.int32) & (LANES - 1)
        turned = [
            halves(pick_lanes(spread_ref[at, k * LANES : (k + 1) * LANES], index))
            for k in range(pieces)
        ]
        step = step.astype(bf16)
        after, here = step < LANES, step == LANES
        value = []
        for k in range(pieces + 1):
            past = turned[pieces - 1 - k] if k < pieces else (zero, zero)
            upto = turned[pieces - k] if k > 0 else (zero, zero)
            value += [jnp.where(after, a, b) for a, b in zip(past, upto)]
        chosen = row_ids == row
        onto = chosen.astype(jnp.float32).astype(bf16)
        acc += jnp.dot(
            onto, jnp.concatenate(value, axis=1), preferred_element_type=jnp.float32
        )
        onto = jnp.concatenate(halves(jnp.where(chosen, ends_at[:, at], 0.0)), axis=0)
        ends += jnp.dot(onto, jnp.where(here, one, zero), preferred_element_type=jnp.float32)

    span_rows, wing_rows = SPAN // LANES, pieces // 2
    shift = (HOP + 1) * span_rows - HOP * span_rows - wing_rows
    acc_ref[...] = jnp.zeros_like(acc_ref)
    acc_ref[shift : shift + rows] = ends[:rows] + ends[rows:]
    for k in range(pieces + 1):
        part = acc[:, 2 * k * LANES : (2 * k + 1) * LANES] + acc[:, (2 * k + 1) * LANES : 2 * (k + 1) * LANES]
        acc_ref[shift + k : shift + k + rows] += part
    odd = lax.rem(lax.axis_index(AXES), 2)
    far = HOP + 1
    give = pl.multiple_of((1 - odd) * (far + 1) * span_rows, span_rows)
    keep = pl.multiple_of(odd * far * span_rows, span_rows)
    give_ref[...] = acc_ref[pl.ds(give, far * span_rows)]
    half_ref[...] = acc_ref[pl.ds(keep, (far + 1) * span_rows)]


def span_sums(line_bin, line_slot, strength, line_count, gauss, lorentz, mixing, factor):
    lines, slots = line_bin.shape[0], gauss.shape[0]
    span_rows = SPAN // LANES
    rows = -(-((2 * HOP + 3) * span_rows + LANES) // 16) * 16
    vmem = pl.BlockSpec(memory_space=pltpu.VMEM)
    return pl.pallas_call(
        deposit_kernel,
        out_shape=[
            pltpu.VMEM(((HOP + 1) * span_rows, LANES), jnp.float32),
            pltpu.VMEM(((HOP + 2) * span_rows, LANES), jnp.float32),
        ],
        in_specs=[pl.BlockSpec(memory_space=pltpu.SMEM)] + [vmem] * 7,
        out_specs=[vmem] * 2,
        scratch_shapes=[
            pltpu.VMEM((rows, LANES), jnp.float32),
            pltpu.VMEM((lines, factor.shape[1] - 1 + LANES), jnp.float32),
        ],
    )(
        line_count,
        line_bin.reshape(1, lines),
        line_slot.reshape(1, lines),
        strength.reshape(1, lines),
        gauss.reshape(1, slots),
        lorentz.reshape(1, slots),
        mixing.reshape(1, slots),
        factor,
    )


def exchanges(groups, members):
    count = groups * members
    pair = [(i, i ^ 1) for i in range(count)]
    near, far, cross = [], [], []
    for i in range(count):
        step = 1 if i % 2 else -1
        end = 0 if i % 2 else members - 1
        for moves, j in ((near, i + step), (far, i + 3 * step)):
            if 0 <= j < count:
                if i // members == j // members:
                    moves.append((i, j))
                elif j % members == end:
                    (far if moves is far else cross).append((i, j))
    return pair, near, far, cross


def body(line_bin, line_slot, strength, line_count, gauss, lorentz, mixing, factor):
    groups, members = lax.axis_size("grp"), lax.axis_size("dev")
    pair, near, far, cross = exchanges(groups, members)
    rows = SPAN // LANES
    even = lax.axis_index("dev") % 2 == 0

    def part(value, first):
        return value[first * rows : (first + 1) * rows]

    give, half = span_sums(line_bin, line_slot, strength, line_count, gauss, lorentz, mixing, factor)
    got = lax.ppermute(give, AXES, pair)
    zero = jnp.zeros((rows, LANES), jnp.float32)
    half = half + jnp.where(
        even, jnp.concatenate([zero, got], axis=0), jnp.concatenate([got, zero], axis=0)
    )
    near = lax.ppermute(half[rows : 3 * rows], AXES, near)
    far = lax.ppermute(jnp.where(even, part(half, 0), part(half, 3)), AXES, far)
    cross = lax.ppermute(jnp.where(even, part(half, 2), part(half, 1)), AXES, cross)
    own = jnp.where(even, part(half, 3) + part(near, 0), part(half, 0) + part(near, 1))
    own = own + far + cross
    other = jnp.where(even, part(near, 1), part(near, 0))
    got = lax.ppermute(other, AXES, pair)
    return (own + got).reshape(SPAN)


def solution(mesh):
    in_specs = (P(AXES),) * 4 + (P(),) * 4
    return jax.shard_map(body, mesh=mesh, in_specs=in_specs, out_specs=P(AXES), check_vma=False)
```

profile of v0, /device:TPU:29, one launch (start us, length us, event | category | flops | bytes accessed | tf_op | source)
XLA Modules:
  0.0 16.4 jit_solution(18222936367912497826)
XLA Ops:
  0.7 3.0 %shard_map.82 = (f32[24,128]{1,0:T(8,128)S(1)}, f32[32,128]{1,0:T(8,128)S(1)}) custom-call(s32[1]{0:T(128)S(6)} %copy.9.count_ref, s32[1,2048]{1,0:T(1,128)} %bitcast.8, s32[1,2048]{1,0:T(1,128)} %bitcast.9, f32[1,2048]{1,0:T(1,128)} %bitcast.10, f32[1,32]{1,0:T(1,128)} %bitcast.11, f32[1,32]{1,0:T(1,128)} %bitcast.12, f32[1,32]{1,0:T(1,128)} %bitcast.13, ...), custom_call_target="tpu_custom_call" | custom-call | tf_op jit(solution)/shard_map/pallas_call | solution.py:159
  3.7 0.7 %collective-permute-start = (f32[24,128]{1,0:T(8,128)S(1)}, f32[24,128]{1,0:T(8,128)S(1)}, u32[]{:S(2)}, u32[]{:S(2)}) collective-permute-start(f32[24,128]{1,0:T(8,128)S(1)} %get-tuple-element.8), channel_id=1, source_target_pairs={{0,1},{1,0},{2,3},{3,2},{4,5},{5,4},{6,7},{7,6},{8,9},{9,8},{10,11... | collective-permute-start | bytes 36872 | tf_op jit(solution)/shard_map/ppermute | solution.py:209
  4.4 0.8 %collective-permute-done = f32[24,128]{1,0:T(8,128)S(1)} collective-permute-done((f32[24,128]{1,0:T(8,128)S(1)}, f32[24,128]{1,0:T(8,128)S(1)}, u32[]{:S(2)}, u32[]{:S(2)}) %collective-permute-start) | collective-permute-done | bytes 12320 | tf_op jit(solution)/shard_map/ppermute | solution.py:209
  5.3 0.6 %collective-permute-start.1 = (f32[16,128]{1,0:T(8,128)S(1)}, f32[16,128]{1,0:T(8,128)S(1)}, u32[]{:S(2)}, u32[]{:S(2)}) collective-permute-start(f32[16,128]{1,0:T(8,128)S(1)} %slice.33), channel_id=1, source_target_pairs={{1,2},{2,1},{3,4},{4,3},{5,6},{6,5},{7,8},{8,7},{9,10},{10,9},{11,... | collective-permute-start | bytes 24584 | tf_op jit(solution)/shard_map/ppermute | solution.py:214
  6.0 1.3 %collective-permute-start.2 = (f32[8,128]{1,0:T(8,128)S(1)}, f32[8,128]{1,0:T(8,128)S(1)}, u32[]{:S(2)}, u32[]{:S(2)}) collective-permute-start(f32[8,128]{1,0:T(8,128)S(1)} %get-tuple-element.9), channel_id=1, source_target_pairs={{1,4},{3,6},{4,1},{5,8},{6,3},{7,10},{8,5},{9,12},{10,7},{11,14},{... | collective-permute-start | bytes 12296 | tf_op jit(solution)/shard_map/ppermute | solution.py:215
  7.3 3.0 %collective-permute-start.3 = (f32[8,128]{1,0:T(8,128)S(1)}, f32[8,128]{1,0:T(8,128)S(1)}, u32[]{:S(2)}, u32[]{:S(2)}) collective-permute-start(f32[8,128]{1,0:T(8,128)S(1)} %get-tuple-element.10), channel_id=1, source_target_pairs={{15,16},{16,15}} | collective-permute-start | bytes 12296 | tf_op jit(solution)/shard_map/ppermute | solution.py:216
  10.2 0.0 collective-permute-done.1
  10.2 1.7 %collective-permute-start.4 = (f32[8,128]{1,0:T(8,128)S(1)}, f32[8,128]{1,0:T(8,128)S(1)}, u32[]{:S(2)}, u32[]{:S(2)}) collective-permute-start(f32[8,128]{1,0:T(8,128)S(1)} %slice_select_fusion.1), channel_id=1, source_target_pairs={{0,1},{1,0},{2,3},{3,2},{4,5},{5,4},{6,7},{7,6},{8,9},{9,8},{10,11... | collective-permute-start | bytes 12296 | tf_op jit(solution)/shard_map/ppermute | solution.py:220
  11.9 1.7 %collective-permute-done.2 = f32[8,128]{1,0:T(8,128)S(1)} collective-permute-done((f32[8,128]{1,0:T(8,128)S(1)}, f32[8,128]{1,0:T(8,128)S(1)}, u32[]{:S(2)}, u32[]{:S(2)}) %collective-permute-start.2) | collective-permute-done | bytes 4128 | tf_op jit(solution)/shard_map/ppermute | solution.py:215
  13.6 2.2 %collective-permute-done.3 = f32[8,128]{1,0:T(8,128)S(1)} collective-permute-done((f32[8,128]{1,0:T(8,128)S(1)}, f32[8,128]{1,0:T(8,128)S(1)}, u32[]{:S(2)}, u32[]{:S(2)}) %collective-permute-start.3) | collective-permute-done | bytes 4128 | tf_op jit(solution)/shard_map/ppermute | solution.py:216
  15.8 0.0 collective-permute-done.4
  15.8 0.6 %add_bitcast_fusion = f32[1024]{0:T(1024)} fusion(f32[8,128]{1,0:T(8,128)S(1)} %collective-permute-done.4, f32[8,128]{1,0:T(8,128)S(1)} %collective-permute-done.3, f32[8,128]{1,0:T(8,128)S(1)} %collective-permute-done.2, f32[16,128]{1,0:T(8,128)S(1)} %collective-permute-done.1, f32[32,128]{1,0:T(8,128)S(1)} %select_add_fusion, pred[]{:T(512)S(6)} %eq.5), kind=kLoop, calls=%fused_computation.2 | loop fusion | flops 6144 | bytes 32769 | tf_op jit(solution)/shard_map/reshape | solution.py:221
  (4 shorter events, 0.0 us)
Async XLA Ops:
  3.7 1.6 %collective-permute-start = (f32[24,128]{1,0:T(8,128)S(1)}, f32[24,128]{1,0:T(8,128)S(1)}, u32[]{:S(2)}, u32[]{:S(2)}) collective-permute-start(f32[24,128]{1,0:T(8,128)S(1)} %get-tuple-element.8), channel_id=1, source_target_pairs={{0,1},{1,0},{2,3},{3,2},{4,5},{5,4},{6,7},{7,6},{8,9},{9,8},{10,11... | collective-permute-start | bytes 36872 | tf_op jit(solution)/shard_map/ppermute | solution.py:209
  5.3 4.9 %collective-permute-start.1 = (f32[16,128]{1,0:T(8,128)S(1)}, f32[16,128]{1,0:T(8,128)S(1)}, u32[]{:S(2)}, u32[]{:S(2)}) collective-permute-start(f32[16,128]{1,0:T(8,128)S(1)} %slice.33), channel_id=1, source_target_pairs={{1,2},{2,1},{3,4},{4,3},{5,6},{6,5},{7,8},{8,7},{9,10},{10,9},{11,... | collective-permute-start | bytes 24584 | tf_op jit(solution)/shard_map/ppermute | solution.py:214
  6.0 7.6 %collective-permute-start.2 = (f32[8,128]{1,0:T(8,128)S(1)}, f32[8,128]{1,0:T(8,128)S(1)}, u32[]{:S(2)}, u32[]{:S(2)}) collective-permute-start(f32[8,128]{1,0:T(8,128)S(1)} %get-tuple-element.9), channel_id=1, source_target_pairs={{1,4},{3,6},{4,1},{5,8},{6,3},{7,10},{8,5},{9,12},{10,7},{11,14},{... | collective-permute-start | bytes 12296 | tf_op jit(solution)/shard_map/ppermute | solution.py:215
  7.3 8.5 %collective-permute-start.3 = (f32[8,128]{1,0:T(8,128)S(1)}, f32[8,128]{1,0:T(8,128)S(1)}, u32[]{:S(2)}, u32[]{:S(2)}) collective-permute-start(f32[8,128]{1,0:T(8,128)S(1)} %get-tuple-element.10), channel_id=1, source_target_pairs={{15,16},{16,15}} | collective-permute-start | bytes 12296 | tf_op jit(solution)/shard_map/ppermute | solution.py:216
  10.2 5.5 %collective-permute-start.4 = (f32[8,128]{1,0:T(8,128)S(1)}, f32[8,128]{1,0:T(8,128)S(1)}, u32[]{:S(2)}, u32[]{:S(2)}) collective-permute-start(f32[8,128]{1,0:T(8,128)S(1)} %slice_select_fusion.1), channel_id=1, source_target_pairs={{0,1},{1,0},{2,3},{3,2},{4,5},{5,4},{6,7},{7,6},{8,9},{9,8},{10,11... | collective-permute-start | bytes 12296 | tf_op jit(solution)/shard_map/ppermute | solution.py:220
where the time goes:
time: 16.6 us; the launch traced here: 16.4 us
  starting transfers between devices  7.31 us (44%)
  waiting for transfers between devices  4.7 us (28%)
  Pallas kernels  3.04 us (18%)
  between operations  0.71 us (4%)
  other arithmetic  0.62 us (4%)
    pallas_call x1, Pallas kernels, span_sums(): pl.pallas_call(deposit_kernel, out_shape=[pltpu.VMEM(((HOP + 1) * span_ro...  3.04 us
    ppermute x1, starting transfers between devices, body(): lax.ppermute(jnp.where(even, part(half, 2), part(half, 1)), AXES, cross)  2.95 us
    ppermute x1, waiting for transfers between devices, body(): lax.ppermute(jnp.where(even, part(half, 2), part(half, 1)), AXES, cross)  2.2 us
    ppermute x1, starting transfers between devices, body(): got = lax.ppermute(other, AXES, pair)  1.67 us
    ppermute x1, waiting for transfers between devices, body(): far = lax.ppermute(jnp.where(even, part(half, 0), part(half, 3)), AXES, far)  1.66 us
    ppermute x1, starting transfers between devices, body(): far = lax.ppermute(jnp.where(even, part(half, 0), part(half, 3)), AXES, far)  1.29 us
    ppermute x1, waiting for transfers between devices, body(): got = lax.ppermute(give, AXES, pair)  0.83 us
    ppermute x1, starting transfers between devices, body(): got = lax.ppermute(give, AXES, pair)  0.74 us
  transfers between devices with their start and end apart: 5, of which 3 were waited for; matrix products, arithmetic and copies ran while one was open for 0% of the time, Pallas kernels for 0%

commit v1 on v0

--- a/solution.py
+++ b/solution.py
@@ -75,14 +75,14 @@
         column(gauss_ref[...]), column(lorentz_ref[...]), column(mixing_ref[...]), factor_ref
     )
     high, low = halves(table)
-    weights = jnp.concatenate([high, low, high], axis=0)
+    weights = jnp.concatenate([high, low, high, low], axis=0)
     aux = lax.broadcasted_iota(jnp.int32, (16, LANES), 0)
     aux_lane = lax.broadcasted_iota(jnp.int32, (16, LANES), 1)
     steps = jnp.where(aux == 0, 1, jnp.where(aux == 1, LANES - aux_lane, 0))
     steps = steps.astype(jnp.float32).astype(bf16)
     weights = jnp.concatenate(
         [
-            jnp.concatenate([weights, jnp.zeros((3 * slots, LANES), bf16)], axis=1),
+            jnp.concatenate([weights, jnp.zeros((4 * slots, LANES), bf16)], axis=1),
             jnp.concatenate([jnp.zeros((16, table.shape[1]), bf16), steps], axis=1),
         ],
         axis=0,
@@ -105,7 +105,7 @@
         chosen_high, chosen_low = halves(chosen)
         aux = jnp.where(aux_ids == 0, col, jnp.where(aux_ids == 1, 1, 0))
         aux = aux.astype(jnp.float32).astype(bf16)
-        picks = jnp.concatenate([chosen_high, chosen_high, chosen_low, aux], axis=0)
+        picks = jnp.concatenate([chosen_high, chosen_high, chosen_low, chosen_low, aux], axis=0)
         spread_ref[at, :] = lax.dot_general(
             picks, weights, (((0,), (0,)), ((), ())), preferred_element_type=jnp.float32
         )

time: 16.6 us -> 16.8 us (1.012)
  Pallas kernels: 3.04 us -> 3.22 us
    pallas_call x1, Pallas kernels: 3.04 us -> 3.22 us  [span_sums(): pl.pallas_call(deposit_kernel, out_shape=[pltpu.VMEM(((HOP + 1) * span_ro...]
where the time goes in v1:
time: 16.8 us; the launch traced here: 16.6 us
  starting transfers between devices  7.31 us (44%)
  waiting for transfers between devices  4.7 us (28%)
  Pallas kernels  3.22 us (19%)
  between operations  0.71 us (4%)
  other arithmetic  0.62 us (4%)
    pallas_call x1, Pallas kernels, span_sums(): pl.pallas_call(deposit_kernel, out_shape=[pltpu.VMEM(((HOP + 1) * span_ro...  3.22 us
    ppermute x1, starting transfers between devices, body(): lax.ppermute(jnp.where(even, part(half, 2), part(half, 1)), AXES, cross)  2.96 us
    ppermute x1, waiting for transfers between devices, body(): lax.ppermute(jnp.where(even, part(half, 2), part(half, 1)), AXES, cross)  2.2 us
    ppermute x1, starting transfers between devices, body(): got = lax.ppermute(other, AXES, pair)  1.67 us
    ppermute x1, waiting for transfers between devices, body(): far = lax.ppermute(jnp.where(even, part(half, 0), part(half, 3)), AXES, far)  1.66 us
    ppermute x1, starting transfers between devices, body(): far = lax.ppermute(jnp.where(even, part(half, 0), part(half, 3)), AXES, far)  1.29 us
    ppermute x1, waiting for transfers between devices, body(): got = lax.ppermute(give, AXES, pair)  0.83 us
    ppermute x1, starting transfers between devices, body(): got = lax.ppermute(give, AXES, pair)  0.74 us
  transfers between devices with their start and end apart: 5, of which 3 were waited for; matrix products, arithmetic and copies ran while one was open for 0% of the time, Pallas kernels for 0%

profile of v1, /device:TPU:29, one launch (start us, length us, event | category | flops | bytes accessed | tf_op | source)
XLA Modules:
  0.0 16.6 jit_solution(14858388952548345766)
XLA Ops:
  0.7 3.2 %shard_map.82 = (f32[24,128]{1,0:T(8,128)S(1)}, f32[32,128]{1,0:T(8,128)S(1)}) custom-call(s32[1]{0:T(128)S(6)} %copy.9.count_ref, s32[1,2048]{1,0:T(1,128)} %bitcast.8, s32[1,2048]{1,0:T(1,128)} %bitcast.9, f32[1,2048]{1,0:T(1,128)} %bitcast.10, f32[1,32]{1,0:T(1,128)} %bitcast.11, f32[1,32]{1,0:T(1,128)} %bitcast.12, f32[1,32]{1,0:T(1,128)} %bitcast.13, ...), custom_call_target="tpu_custom_call" | custom-call | tf_op jit(solution)/shard_map/pallas_call | solution.py:159
  3.9 0.7 %collective-permute-start = (f32[24,128]{1,0:T(8,128)S(1)}, f32[24,128]{1,0:T(8,128)S(1)}, u32[]{:S(2)}, u32[]{:S(2)}) collective-permute-start(f32[24,128]{1,0:T(8,128)S(1)} %get-tuple-element.8), channel_id=1, source_target_pairs={{0,1},{1,0},{2,3},{3,2},{4,5},{5,4},{6,7},{7,6},{8,9},{9,8},{10,11... | collective-permute-start | bytes 36872 | tf_op jit(solution)/shard_map/ppermute | solution.py:209
  4.6 0.8 %collective-permute-done = f32[24,128]{1,0:T(8,128)S(1)} collective-permute-done((f32[24,128]{1,0:T(8,128)S(1)}, f32[24,128]{1,0:T(8,128)S(1)}, u32[]{:S(2)}, u32[]{:S(2)}) %collective-permute-start) | collective-permute-done | bytes 12320 | tf_op jit(solution)/shard_map/ppermute | solution.py:209
  5.5 0.6 %collective-permute-start.1 = (f32[16,128]{1,0:T(8,128)S(1)}, f32[16,128]{1,0:T(8,128)S(1)}, u32[]{:S(2)}, u32[]{:S(2)}) collective-permute-start(f32[16,128]{1,0:T(8,128)S(1)} %slice.33), channel_id=1, source_target_pairs={{1,2},{2,1},{3,4},{4,3},{5,6},{6,5},{7,8},{8,7},{9,10},{10,9},{11,... | collective-permute-start | bytes 24584 | tf_op jit(solution)/shard_map/ppermute | solution.py:214
  6.1 1.3 %collective-permute-start.2 = (f32[8,128]{1,0:T(8,128)S(1)}, f32[8,128]{1,0:T(8,128)S(1)}, u32[]{:S(2)}, u32[]{:S(2)}) collective-permute-start(f32[8,128]{1,0:T(8,128)S(1)} %get-tuple-element.9), channel_id=1, source_target_pairs={{1,4},{3,6},{4,1},{5,8},{6,3},{7,10},{8,5},{9,12},{10,7},{11,14},{... | collective-permute-start | bytes 12296 | tf_op jit(solution)/shard_map/ppermute | solution.py:215
  7.4 3.0 %collective-permute-start.3 = (f32[8,128]{1,0:T(8,128)S(1)}, f32[8,128]{1,0:T(8,128)S(1)}, u32[]{:S(2)}, u32[]{:S(2)}) collective-permute-start(f32[8,128]{1,0:T(8,128)S(1)} %get-tuple-element.10), channel_id=1, source_target_pairs={{15,16},{16,15}} | collective-permute-start | bytes 12296 | tf_op jit(solution)/shard_map/ppermute | solution.py:216
  10.4 0.0 collective-permute-done.1
  10.4 1.7 %collective-permute-start.4 = (f32[8,128]{1,0:T(8,128)S(1)}, f32[8,128]{1,0:T(8,128)S(1)}, u32[]{:S(2)}, u32[]{:S(2)}) collective-permute-start(f32[8,128]{1,0:T(8,128)S(1)} %slice_select_fusion.1), channel_id=1, source_target_pairs={{0,1},{1,0},{2,3},{3,2},{4,5},{5,4},{6,7},{7,6},{8,9},{9,8},{10,11... | collective-permute-start | bytes 12296 | tf_op jit(solution)/shard_map/ppermute | solution.py:220
  12.1 1.7 %collective-permute-done.2 = f32[8,128]{1,0:T(8,128)S(1)} collective-permute-done((f32[8,128]{1,0:T(8,128)S(1)}, f32[8,128]{1,0:T(8,128)S(1)}, u32[]{:S(2)}, u32[]{:S(2)}) %collective-permute-start.2) | collective-permute-done | bytes 4128 | tf_op jit(solution)/shard_map/ppermute | solution.py:215
  13.8 2.2 %collective-permute-done.3 = f32[8,128]{1,0:T(8,128)S(1)} collective-permute-done((f32[8,128]{1,0:T(8,128)S(1)}, f32[8,128]{1,0:T(8,128)S(1)}, u32[]{:S(2)}, u32[]{:S(2)}) %collective-permute-start.3) | collective-permute-done | bytes 4128 | tf_op jit(solution)/shard_map/ppermute | solution.py:216
  16.0 0.0 collective-permute-done.4
  16.0 0.6 %add_bitcast_fusion = f32[1024]{0:T(1024)} fusion(f32[8,128]{1,0:T(8,128)S(1)} %collective-permute-done.4, f32[8,128]{1,0:T(8,128)S(1)} %collective-permute-done.3, f32[8,128]{1,0:T(8,128)S(1)} %collective-permute-done.2, f32[16,128]{1,0:T(8,128)S(1)} %collective-permute-done.1, f32[32,128]{1,0:T(8,128)S(1)} %select_add_fusion, pred[]{:T(512)S(6)} %eq.5), kind=kLoop, calls=%fused_computation.2 | loop fusion | flops 6144 | bytes 32769 | tf_op jit(solution)/shard_map/reshape | solution.py:221
  (4 shorter events, 0.0 us)
Async XLA Ops:
  3.9 1.6 %collective-permute-start = (f32[24,128]{1,0:T(8,128)S(1)}, f32[24,128]{1,0:T(8,128)S(1)}, u32[]{:S(2)}, u32[]{:S(2)}) collective-permute-start(f32[24,128]{1,0:T(8,128)S(1)} %get-tuple-element.8), channel_id=1, source_target_pairs={{0,1},{1,0},{2,3},{3,2},{4,5},{5,4},{6,7},{7,6},{8,9},{9,8},{10,11... | collective-permute-start | bytes 36872 | tf_op jit(solution)/shard_map/ppermute | solution.py:209
  5.5 4.9 %collective-permute-start.1 = (f32[16,128]{1,0:T(8,128)S(1)}, f32[16,128]{1,0:T(8,128)S(1)}, u32[]{:S(2)}, u32[]{:S(2)}) collective-permute-start(f32[16,128]{1,0:T(8,128)S(1)} %slice.33), channel_id=1, source_target_pairs={{1,2},{2,1},{3,4},{4,3},{5,6},{6,5},{7,8},{8,7},{9,10},{10,9},{11,... | collective-permute-start | bytes 24584 | tf_op jit(solution)/shard_map/ppermute | solution.py:214
  6.1 7.6 %collective-permute-start.2 = (f32[8,128]{1,0:T(8,128)S(1)}, f32[8,128]{1,0:T(8,128)S(1)}, u32[]{:S(2)}, u32[]{:S(2)}) collective-permute-start(f32[8,128]{1,0:T(8,128)S(1)} %get-tuple-element.9), channel_id=1, source_target_pairs={{1,4},{3,6},{4,1},{5,8},{6,3},{7,10},{8,5},{9,12},{10,7},{11,14},{... | collective-permute-start | bytes 12296 | tf_op jit(solution)/shard_map/ppermute | solution.py:215
  7.4 8.5 %collective-permute-start.3 = (f32[8,128]{1,0:T(8,128)S(1)}, f32[8,128]{1,0:T(8,128)S(1)}, u32[]{:S(2)}, u32[]{:S(2)}) collective-permute-start(f32[8,128]{1,0:T(8,128)S(1)} %get-tuple-element.10), channel_id=1, source_target_pairs={{15,16},{16,15}} | collective-permute-start | bytes 12296 | tf_op jit(solution)/shard_map/ppermute | solution.py:216
  10.4 5.5 %collective-permute-start.4 = (f32[8,128]{1,0:T(8,128)S(1)}, f32[8,128]{1,0:T(8,128)S(1)}, u32[]{:S(2)}, u32[]{:S(2)}) collective-permute-start(f32[8,128]{1,0:T(8,128)S(1)} %slice_select_fusion.1), channel_id=1, source_target_pairs={{0,1},{1,0},{2,3},{3,2},{4,5},{5,4},{6,7},{7,6},{8,9},{9,8},{10,11... | collective-permute-start | bytes 12296 | tf_op jit(solution)/shard_map/ppermute | solution.py:220
